TPU v7x, 32 devices: a whole 2x2x4 slice. The times are simulated.
32 devices in a mesh: grp: 2 (over y), vec: 4 (over z), occ: 2 (over x), wlk: 2 (over core).
Axes of the slice: x: 2, y: 2, z: 4, core: 2. Of those that a mesh axis runs over, the one named last changes fastest.
Arguments:
- chol_half: bfloat16 [256, 256, 2048], P(('grp', 'vec'), 'occ'), parts along dimension 0, may hold values from -0.046875 to 0.046875
- theta: bfloat16 [8, 2048, 256], P(('grp', 'wlk'), 'vec', 'occ'), parts along dimension 0, may hold values from -6 to 6
Outputs:
- theta_grad: float32 [8, 2048, 256], P(('grp', 'wlk'), 'vec', 'occ'), parts along dimension 0
There are 2 independent parts, one for each index of `grp`. A program takes and returns all parts, laid end to end along the dimension named above; each array names one. Nothing has to cross between parts.
All inputs are finite; a program needn't handle non-finite values.
Results may differ from a plain program's by a relative error of at most 0.0042.
Values may be sent and summed in bfloat16 or wider, within the bound.
A program may use at most 64 MiB of HBM per device.

v0:
```python
import jax
import jax.numpy as jnp
from jax import lax
from jax.sharding import PartitionSpec as P


def on_device(chol_half, theta):
    widened = lax.all_gather(theta, "occ", axis=2, tiled=True)
    factor_rows = chol_half
    amplitude_sums = jnp.einsum(
        "gip,wpj->wgij",
        factor_rows,
        lax.all_gather(widened, "vec", axis=1, tiled=True),
        preferred_element_type=jnp.float32,
    )
    amplitudes = amplitude_sums.astype(jnp.bfloat16)
    swapped = lax.all_to_all(amplitudes, "occ", split_axis=3, concat_axis=2, tiled=True)
    factor_rows = chol_half
    summed_rows = lax.psum_scatter(
        jnp.einsum("gap,wgba->pwb", factor_rows, swapped, preferred_element_type=jnp.float32),
        "vec",
        scatter_dimension=0,
        tiled=True,
    )
    owned = lax.psum_scatter(summed_rows, "occ", scatter_dimension=2, tiled=True)
    return -jnp.transpose(owned, (1, 0, 2))


def solution(mesh):
    placed = (P(("grp", "vec"), "occ", None), P(("grp", "wlk"), "vec", "occ"))
    return jax.shard_map(
        on_device,
        mesh=mesh,
        in_specs=placed,
        out_specs=P(("grp", "wlk"), "vec", "occ"),
        check_vma=False,
    )
```

profile of v0, /device:TPU:26, one launch (start us, length us, event | category | flops | bytes accessed | tf_op | source)
XLA Modules:
  0.0 257.1 jit_solution(8337746905256795681)
XLA Ops:
  6.5 0.0 all-gather.2.cloned.1.call-start
  6.5 1.1 copy.6
  7.6 8.8 %all_gather.6 = bf16[2,512,256]{1,2,0:T(8,128)(2,1)} all-gather(bf16[2,512,128]{1,2,0:T(8,128)(2,1)S(1)} %copy.6), channel_id=1, replica_groups=mesh['grp'=2,'vec'=4,'occ'=2,'wlk'=2] {'occ'}, dimensions={2}, use_global_device_ids=true | all-gather | bytes 786432 | tf_op jit(solution)/shard_map/all_gather | solution.py:8
  16.4 0.0 all-gather.2.cloned.1.call-update
  16.5 0.0 reduce-scatter.3.cloned.1.call-start
  16.5 44.5 %all-gather.2.cloned.1.call-done = bf16[2,2048,256]{1,2,0:T(8,128)(2,1)} async-done(((bf16[2,512,256]{1,2,0:T(8,128)(2,1)}), bf16[2,2048,256]{1,2,0:T(8,128)(2,1)}) %all-gather.2.cloned.1.call-update) | async-done | bytes 2097168 | tf_op jit(solution)/shard_map/all_gather | solution.py:13
  61.1 12.4 %convert_bitcast_fusion = bf16[2,32,128,256]{2,3,1,0:T(8,128)(2,1)S(1)} fusion(bf16[32,128,2048]{2,1,0:T(8,128)(2,1)} %param.2, bf16[2,2048,256]{1,2,0:T(8,128)(2,1)} %all-gather.2.cloned.1.call-done), kind=kOutput, calls=%fused_computation.4 | convolution fusion | flops 8592031744 | bytes 23068672 | tf_op jit(solution)/shard_map/gip,wpj->wgij/dot_general | solution.py:10
  73.5 2.7 %copy.7 = bf16[2,32,128,256]{2,1,0,3:T(8,128)(2,1)S(1)} copy(bf16[2,32,128,256]{2,3,1,0:T(8,128)(2,1)S(1)} %convert_bitcast_fusion) | data formatting | bytes 8388608 | tf_op jit(solution)/shard_map/convert_element_type | solution.py:16
  76.2 50.5 %all_to_all.18 = bf16[2,32,128,256]{2,1,0,3:T(8,128)(2,1)} all-to-all(bf16[2,32,128,256]{2,1,0,3:T(8,128)(2,1)S(1)} %copy.7), channel_id=1, replica_groups=mesh['grp'=2,'vec'=4,'occ'=2,'wlk'=2] {'occ'}, dimensions={3} | all-to-all | bytes 8388608 | tf_op jit(solution)/shard_map/all_to_all | solution.py:17
  126.7 7.5 %copy.8 = bf16[2,32,128,2,128]{4,2,3,1,0:T(8,128)(2,1)} copy(bf16[2,32,128,2,128]{2,1,0,4,3:T(8,128)(2,1)} %bitcast.28) | data formatting | bytes 8388608 | tf_op jit(solution)/shard_map/all_to_all | solution.py:17
  134.2 14.1 %fusion.4 = f32[2048,2,256]{0,2,1:T(8,128)} fusion(bf16[2,32,256,128]{3,2,1,0:T(8,128)(2,1)} %bitcast.29, bf16[32,128,2048]{2,1,0:T(8,128)(2,1)} %param.2), kind=kOutput, calls=%fused_computation.5 | convolution fusion | flops 8589934592 | bytes 25165824 | tf_op jit(solution)/shard_map/gap,wgba->pwb/dot_general | solution.py:20
  148.4 0.0 reduce-scatter.3.cloned.1.call-update
  148.4 0.0 reduce-scatter.5.cloned.1.call-start
  148.4 77.3 %reduce-scatter.3.cloned.1.call-done = f32[512,2,256]{0,2,1:T(8,128)} async-done(((f32[2048,2,256]{0,2,1:T(8,128)}), f32[512,2,256]{0,2,1:T(8,128)}) %reduce-scatter.3.cloned.1.call-update) | async-done | bytes 1048592 | tf_op jit(solution)/shard_map/reduce_scatter | solution.py:19
  225.7 0.0 reduce-scatter.5.cloned.1.call-update
  225.7 22.8 %reduce-scatter.5.cloned.1.call-done = f32[512,2,128]{0,2,1:T(8,128)} async-done(((f32[512,2,256]{0,2,1:T(8,128)}), f32[512,2,128]{0,2,1:T(8,128)}) %reduce-scatter.5.cloned.1.call-update) | async-done | bytes 524304 | tf_op jit(solution)/shard_map/reduce_scatter | solution.py:25
  248.5 1.1 negate_bitcast_fusion
  249.6 1.0 copy.9
Async XLA Ops:
  6.5 54.5 %all-gather.2.cloned.1.call-start = ((), (), s32[]{:S(2)}) async-start(), calls=%async_computation.3 | async-start | bytes 2621440 | tf_op jit(solution)/shard_map/all_gather | solution.py:13
  16.5 209.2 %reduce-scatter.3.cloned.1.call-start = ((), (), s32[]{:S(2)}) async-start(), calls=%async_computation.4 | async-start | bytes 5242880 | tf_op jit(solution)/shard_map/reduce_scatter | solution.py:19
  148.4 100.1 %reduce-scatter.5.cloned.1.call-start = ((), (), s32[]{:S(2)}) async-start(), calls=%async_computation.5 | async-start | bytes 1572864 | tf_op jit(solution)/shard_map/reduce_scatter | solution.py:25
Sparse Core Ops, SparseCore 0:
  16.6 44.4 all-gather.1
  148.5 77.1 reduce-scatter.2
  227.9 20.4 reduce-scatter.4
where the time goes:
time: 260 us; the launch traced here: 257 us
  waiting for transfers between devices  145 us (56%)
  blocking collectives  59.4 us (23%)
  matrix products  26.5 us (10%)
  between operations  13.1 us (5%)
  local copies, waits for them, and re-layouts  12.3 us (5%)
    reduce_scatter x1, waiting for transfers between devices, on_device(): lax.psum_scatter(jnp.einsum('gap,wgba->pwb', factor_rows, swapped, prefer...  77.3 us
    all_to_all x1, blocking collectives, on_device(): lax.all_to_all(amplitudes, 'occ', split_axis=3, concat_axis=2, tiled=True)  50.5 us
    all_gather x1, waiting for transfers between devices, on_device(): lax.all_gather(widened, 'vec', axis=1, tiled=True)  44.5 us
    reduce_scatter x1, waiting for transfers between devices, on_device(): lax.psum_scatter(summed_rows, 'occ', scatter_dimension=2, tiled=True)  22.8 us
    dot_general x1, matrix products, on_device(): jnp.einsum('gap,wgba->pwb', factor_rows, swapped, preferred_element_type=...  14.1 us
    dot_general x1, matrix products, on_device(): jnp.einsum('gip,wpj->wgij', factor_rows, lax.all_gather(widened, 'vec', a...  12.4 us
    all_gather x1, blocking collectives, on_device(): widened = lax.all_gather(theta, 'occ', axis=2, tiled=True)  8.82 us
    all_to_all x1, local copies, waits for them, and re-layouts, on_device(): lax.all_to_all(amplitudes, 'occ', split_axis=3, concat_axis=2, tiled=True)  7.48 us
  transfers between devices with their start and end apart: 3, of which 3 were waited for; matrix products, arithmetic and copies ran while one was open for 0% of the time, Pallas kernels for 0%

commit v1 on v0

v1 whole, which is shorter than its diff:
```python
import functools

import jax
import jax.numpy as jnp
from jax import lax
from jax.experimental import pallas as pl
from jax.experimental.pallas import tpu as pltpu
from jax.sharding import PartitionSpec as P

MESH = pl.DeviceIdType.MESH
F32 = jnp.float32
BF16 = jnp.bfloat16


def kernel(nz, dims, chol, theta, out, cv, thp, thd, asend, arecv, adiag, accd, accr, gsend, grecv, gown, xs, xr,
           csem, txs, txr, tzs, tzr, ass, asr, gss, gsr, xss, xsr):
    G, R, M, W, Q, CH = dims
    GC = G // CH
    z = lax.axis_index("vec")
    partner = {"occ": 1 - lax.axis_index("occ")}
    peers = [lax.rem(z + k, nz) for k in range(1, nz)]
    mine = pl.ds(pl.multiple_of(z * Q, Q), Q)

    def c_copy(c):
        part = pl.ds(c * GC, GC)
        return pltpu.make_async_copy(chol.at[part], cv.at[part], csem.at[c])

    def remote(src, dst, ss, rs, to):
        return pltpu.make_async_remote_copy(src_ref=src, dst_ref=dst, send_sem=ss, recv_sem=rs, device_id=to, device_id_type=MESH)

    for c in range(CH):
        c_copy(c).start()

    barrier = pltpu.get_barrier_semaphore()
    pl.semaphore_signal(barrier, inc=1, device_id=partner, device_id_type=MESH)
    for peer in peers:
        pl.semaphore_signal(barrier, inc=1, device_id={"vec": peer}, device_id_type=MESH)
    pl.semaphore_wait(barrier, nz)

    def theta_x(w):
        return remote(theta.at[w], thp.at[w, mine], txs.at[w], txr.at[w], partner)

    def rows_of(s):
        return pl.ds(pl.multiple_of(s * Q, Q), Q)

    def theta_p(w, k, s):
        rows = rows_of(s)
        return remote(thp.at[w, rows], thp.at[w, rows], tzs.at[w, k], tzr.at[w, s], {"vec": peers[k]})

    def theta_d(w, k, s):
        return remote(theta.at[w], thd.at[rows_of(s), pl.ds(w * R, R)], tzs.at[W + w, k], tzr.at[W + w, s], {"vec": peers[k]})

    for w in range(W):
        theta_x(w).start()
    for w in range(W):
        theta_x(w).wait_recv()
        for k in range(nz - 1):
            theta_p(w, k, z).start()
    for w in range(W):
        for k in range(nz - 1):
            theta_d(w, k, z).start()
        thd[mine, pl.ds(w * R, R)] = theta[w]

    def a_copy(w, c):
        part = pl.ds(c * GC, GC)
        return remote(asend.at[w, part], arecv.at[w, part], ass.at[w, c], asr.at[w, c], partner)

    for w in range(W):
        for k in range(nz - 1):
            theta_p(w, k, peers[k]).wait_recv()

        @pl.loop(0, CH)
        def _(c):
            if w == 0:
                c_copy(c).wait()
            part = pl.ds(c * GC, GC)
            block = jnp.dot(cv[part].reshape(GC * R, M), thp[w], preferred_element_type=F32)
            asend[w, part] = block.astype(BF16).reshape(GC, R, R)
            a_copy(w, c).start()

    def g_copy(e, k, s, d):
        return remote(gsend.at[e, d], grecv.at[e, s], gss.at[e, k], gsr.at[e, s], {"vec": peers[k]})

    def scatter(e, acc, first):
        rows = pl.ds(first, R)
        for d in range(nz):
            gsend[e, d] = acc[rows, pl.ds(d * Q, Q)].astype(BF16)
        gown[e] = acc[rows, mine]
        for k in range(nz - 1):
            g_copy(e, k, z, peers[k]).start()

    def gathered(e):
        total = gown[e]
        for k in range(nz - 1):
            g_copy(e, k, peers[k], peers[k]).wait_recv()
            total = total + grecv[e, peers[k]].astype(F32)
        return total

    def x_copy(w):
        return remote(xs.at[w], xr.at[w], xss.at[w], xsr.at[w], partner)

    for w in range(W):
        for k in range(nz - 1):
            theta_d(w, k, peers[k]).wait_recv()
    accd[...] = jnp.zeros_like(accd)

    @pl.loop(0, CH)
    def _(c):
        part = pl.ds(c * GC, GC)
        block = jnp.dot(cv[part].reshape(GC * R, M), thd[...], preferred_element_type=F32)
        adiag[part] = block.astype(BF16).reshape(GC, R, W * R)

    def add_chunk(acc, lhs, part):
        for n in range(nz):
            cols = pl.ds(n * Q, Q)
            acc[:, cols] += jnp.dot(lhs, cv[part, :, cols].reshape(GC * R, Q), preferred_element_type=F32)

    @pl.loop(0, CH)
    def _(c):
        part = pl.ds(c * GC, GC)
        block = adiag[part]
        lhs = jnp.concatenate(
            [jnp.concatenate([block[g, :, w * R:(w + 1) * R] for g in range(GC)], axis=1) for w in range(W)], axis=0
        )
        add_chunk(accd, lhs, part)

    for w in range(W):
        if w == 0:
            for v in range(W):
                scatter(v, accd, v * R)
        accr[...] = jnp.zeros_like(accr)

        @pl.loop(0, CH)
        def _(c):
            a_copy(w, c).wait_recv()
            part = pl.ds(c * GC, GC)
            block = arecv[w, part]
            add_chunk(accr, jnp.concatenate([block[g] for g in range(GC)], axis=1), part)

        scatter(W + w, accr, 0)

    for w in range(W):
        gown[w] = gathered(w)
    for w in range(W):
        xs[w] = gathered(W + w).astype(BF16)
        x_copy(w).start()
    for w in range(W):
        x_copy(w).wait_recv()
        out[w] = -(gown[w] + xr[w].astype(F32)).T

    for w in range(W):
        theta_x(w).wait_send()
        x_copy(w).wait_send()
        for k in range(nz - 1):
            theta_p(w, k, z).wait_send()
            theta_d(w, k, z).wait_send()
            g_copy(w, k, z, peers[k]).wait_send()
            g_copy(W + w, k, z, peers[k]).wait_send()

        @pl.loop(0, CH)
        def _(c):
            a_copy(w, c).wait_send()


def fused(nz, chol_half, theta):
    G, R, M = chol_half.shape
    W, Q, _ = theta.shape
    CH = 8 if G % 8 == 0 else 1
    dims = (G, R, M, W, Q, CH)
    dma = pltpu.SemaphoreType.DMA
    return pl.pallas_call(
        functools.partial(kernel, nz, dims),
        out_shape=jax.ShapeDtypeStruct((W, Q, R), F32),
        in_specs=[pl.BlockSpec(memory_space=pl.ANY), pl.BlockSpec(memory_space=pltpu.VMEM)],
        out_specs=pl.BlockSpec(memory_space=pltpu.VMEM),
        scratch_shapes=[
            pltpu.VMEM((G, R, M), BF16),
            pltpu.VMEM((W, M, R), BF16),
            pltpu.VMEM((M, W * R), BF16),
            pltpu.VMEM((W, G, R, R), BF16),
            pltpu.VMEM((W, G, R, R), BF16),
            pltpu.VMEM((G, R, W * R), BF16),
            pltpu.VMEM((W * R, M), F32),
            pltpu.VMEM((R, M), F32),
            pltpu.VMEM((2 * W, nz, R, Q), BF16),
            pltpu.VMEM((2 * W, nz, R, Q), BF16),
            pltpu.VMEM((2 * W, R, Q), F32),
            pltpu.VMEM((W, R, Q), BF16),
            pltpu.VMEM((W, R, Q), BF16),
            dma((CH,)),
            dma((W,)),
            dma((W,)),
            dma((2 * W, nz)),
            dma((2 * W, nz)),
            dma((W, CH)),
            dma((W, CH)),
            dma((2 * W, nz)),
            dma((2 * W, nz)),
            dma((W,)),
            dma((W,)),
        ],
        compiler_params=pltpu.CompilerParams(collective_id=0, has_side_effects=True, vmem_limit_bytes=60 << 20),
    )(chol_half, theta)


def on_device(mesh, chol_half, theta):
    G, R, M = chol_half.shape
    nz = mesh.shape["vec"]
    if mesh.shape["occ"] == 2 and R % 128 == 0 and theta.shape[1] % 128 == 0 and G * R * M <= 8 << 20:
        return fused(nz, chol_half, theta)
    widened = lax.all_gather(theta, "occ", axis=2, tiled=True)
    amplitude_sums = jnp.einsum(
        "gip,wpj->wgij", chol_half, lax.all_gather(widened, "vec", axis=1, tiled=True), preferred_element_type=F32
    )
    amplitudes = amplitude_sums.astype(BF16)
    swapped = lax.all_to_all(amplitudes, "occ", split_axis=3, concat_axis=2, tiled=True)
    summed_rows = lax.psum_scatter(
        jnp.einsum("gap,wgba->pwb", chol_half, swapped, preferred_element_type=F32),
        "vec",
        scatter_dimension=0,
        tiled=True,
    )
    owned = lax.psum_scatter(summed_rows, "occ", scatter_dimension=2, tiled=True)
    return -jnp.transpose(owned, (1, 0, 2))


def solution(mesh):
    return jax.shard_map(
        functools.partial(on_device, mesh),
        mesh=mesh,
        in_specs=(P(("grp", "vec"), "occ", None), P(("grp", "wlk"), "vec", "occ")),
        out_specs=P(("grp", "wlk"), "vec", "occ"),
        check_vma=False,
    )
```

time: 260 us -> 119 us (0.46); the launches traced: 257 us -> 119 us
  waiting for transfers between devices: 145 us -> 0 us
  Pallas kernels: 0 us -> 117 us
  blocking collectives: 59.4 us -> 0 us
  matrix products: 26.5 us -> 0 us
  between operations: 13.1 us -> 0.01 us
  local copies, waits for them, and re-layouts: 12.3 us -> 1.87 us
    pallas_call x0 -> x1, Pallas kernels: none -> 117 us  [fused(): pl.pallas_call(functools.partial(kernel, nz, dims), out_shape=jax.ShapeDt...]
    reduce_scatter x2 -> x0, waiting for transfers between devices: 100 us -> none  [the longest x1 77.3 us: on_device(): lax.psum_scatter(jnp.einsum('gap,wgba->pwb', factor_rows, swapped, prefer...]
    all_to_all x1 -> x0, blocking collectives: 50.5 us -> none  [on_device(): lax.all_to_all(amplitudes, 'occ', split_axis=3, concat_axis=2, tiled=True)]
    all_gather x1 -> x0, waiting for transfers between devices: 44.5 us -> none  [on_device(): lax.all_gather(widened, 'vec', axis=1, tiled=True)]
    dot_general x2 -> x0, matrix products: 26.5 us -> none  [the longest x1 14.1 us: on_device(): jnp.einsum('gap,wgba->pwb', factor_rows, swapped, preferred_element_type=...]
    all_gather x1 -> x0, blocking collectives: 8.82 us -> none  [on_device(): widened = lax.all_gather(theta, 'occ', axis=2, tiled=True)]
    all_to_all x1 -> x0, local copies, waits for them, and re-layouts: 7.48 us -> none  [on_device(): lax.all_to_all(amplitudes, 'occ', split_axis=3, concat_axis=2, tiled=True)]
    convert_element_type x1 -> x0, local copies, waits for them, and re-layouts: 2.7 us -> none  [on_device(): amplitudes = amplitude_sums.astype(jnp.bfloat16)]
  transfers between devices with their start and end apart: 3 -> 0, of which waited for: 3 -> 0; matrix products, arithmetic and copies ran while one was open for 0% -> 0% of each run, Pallas kernels for 0% -> 0%
where the time goes in v1:
time: 119 us
  Pallas kernels  117 us (98%)
  local copies, waits for them, and re-layouts  1.87 us (2%)
    pallas_call x1, Pallas kernels, fused(): pl.pallas_call(functools.partial(kernel, nz, dims), out_shape=jax.ShapeDt...  117 us

profile of v1, /device:TPU:26, one launch (start us, length us, event | category | flops | bytes accessed | tf_op | source)
XLA Modules:
  0.0 119.2 jit_solution(8746273713863125841)
XLA Ops:
  0.0 117.3 %shard_map.28 = f32[2,512,128]{2,1,0:T(8,128)} custom-call(bf16[32,128,2048]{2,1,0:T(8,128)(2,1)} %chol.1, bf16[2,512,128]{2,1,0:T(8,128)(2,1)} %theta.1), custom_call_target="tpu_custom_call" | custom-call | tf_op jit(solution)/shard_map/pallas_call | solution.py:171
  117.3 1.9 %copy.4 = f32[2,512,128]{2,1,0:T(8,128)} copy(f32[2,512,128]{2,1,0:T(8,128)} %shard_map.28) | data formatting | bytes 1048576

commit v2 on v1

--- a/solution.py
+++ b/solution.py
@@ -99,35 +99,12 @@
     def x_copy(w):
         return remote(xs.at[w], xr.at[w], xss.at[w], xsr.at[w], partner)
 
-    for w in range(W):
-        for k in range(nz - 1):
-            theta_d(w, k, peers[k]).wait_recv()
-    accd[...] = jnp.zeros_like(accd)
-
-    @pl.loop(0, CH)
-    def _(c):
-        part = pl.ds(c * GC, GC)
-        block = jnp.dot(cv[part].reshape(GC * R, M), thd[...], preferred_element_type=F32)
-        adiag[part] = block.astype(BF16).reshape(GC, R, W * R)
-
     def add_chunk(acc, lhs, part):
         for n in range(nz):
             cols = pl.ds(n * Q, Q)
             acc[:, cols] += jnp.dot(lhs, cv[part, :, cols].reshape(GC * R, Q), preferred_element_type=F32)
 
-    @pl.loop(0, CH)
-    def _(c):
-        part = pl.ds(c * GC, GC)
-        block = adiag[part]
-        lhs = jnp.concatenate(
-            [jnp.concatenate([block[g, :, w * R:(w + 1) * R] for g in range(GC)], axis=1) for w in range(W)], axis=0
-        )
-        add_chunk(accd, lhs, part)
-
-    for w in range(W):
-        if w == 0:
-            for v in range(W):
-                scatter(v, accd, v * R)
+    def received(w):
         accr[...] = jnp.zeros_like(accr)
 
         @pl.loop(0, CH)
@@ -139,11 +116,37 @@
 
         scatter(W + w, accr, 0)
 
-    for w in range(W):
-        gown[w] = gathered(w)
+    received(0)
+    for w in range(W):
+        for k in range(nz - 1):
+            theta_d(w, k, peers[k]).wait_recv()
+    accd[...] = jnp.zeros_like(accd)
+
+    @pl.loop(0, CH)
+    def _(c):
+        part = pl.ds(c * GC, GC)
+        block = jnp.dot(cv[part].reshape(GC * R, M), thd[...], preferred_element_type=F32)
+        adiag[part] = block.astype(BF16).reshape(GC, R, W * R)
+
+    @pl.loop(0, CH)
+    def _(c):
+        part = pl.ds(c * GC, GC)
+        block = adiag[part]
+        lhs = jnp.concatenate(
+            [jnp.concatenate([block[g, :, w * R:(w + 1) * R] for g in range(GC)], axis=1) for w in range(W)], axis=0
+        )
+        add_chunk(accd, lhs, part)
+
+    for w in range(W):
+        scatter(w, accd, w * R)
+        if w + 1 < W:
+            received(w + 1)
+
     for w in range(W):
         xs[w] = gathered(W + w).astype(BF16)
         x_copy(w).start()
+    for w in range(W):
+        gown[w] = gathered(w)
     for w in range(W):
         x_copy(w).wait_recv()
         out[w] = -(gown[w] + xr[w].astype(F32)).T

time: 119 us -> 107 us (0.90); the launches traced: 119 us -> 105 us
  Pallas kernels: 117 us -> 103 us
    pallas_call x1, Pallas kernels: 117 us -> 103 us  [fused(): pl.pallas_call(functools.partial(kernel, nz, dims), out_shape=jax.ShapeDt...]
where the time goes in v2:
time: 107 us; the launch traced here: 105 us
  Pallas kernels  103 us (96%)
  local copies, waits for them, and re-layouts  1.87 us (2%)
    pallas_call x1, Pallas kernels, fused(): pl.pallas_call(functools.partial(kernel, nz, dims), out_shape=jax.ShapeDt...  103 us

profile of v2, /device:TPU:26, one launch (start us, length us, event | category | flops | bytes accessed | tf_op | source)
XLA Modules:
  0.0 105.2 jit_solution(2619808638277667203)
XLA Ops:
  0.0 103.3 %shard_map.28 = f32[2,512,128]{2,1,0:T(8,128)} custom-call(bf16[32,128,2048]{2,1,0:T(8,128)(2,1)} %chol.1, bf16[2,512,128]{2,1,0:T(8,128)(2,1)} %theta.1), custom_call_target="tpu_custom_call" | custom-call | tf_op jit(solution)/shard_map/pallas_call | solution.py:174
  103.3 1.9 %copy.4 = f32[2,512,128]{2,1,0:T(8,128)} copy(f32[2,512,128]{2,1,0:T(8,128)} %shard_map.28) | data formatting | bytes 1048576
